TPU v7x, 128 devices: a whole 4x4x4 slice. The times are simulated.
128 devices in a mesh: dp: 8 (over x, z_lo), tensor: 16 (over y, z_hi, core).
Axes of the slice: x: 4, y: 4, z: 4 (z_hi: 2, z_lo: 2; z = z_hi * 2 + z_lo), core: 2. Of those that a mesh axis runs over, the one named last changes fastest.
Arguments:
- hidden_act: bfloat16 [5632, 36864], P('dp', 'tensor'), may hold values from -80 to 80
- out_grad: bfloat16 [5632, 4608], P('dp', 'tensor'), may hold values from -0.5 to 0.5
- other_sq: float32 [16], P('dp'), may hold values from 2989699 to 597939968
Outputs:
- weight_grad: float32 [4608, 36864], P('dp', 'tensor')
All inputs are finite; a program needn't handle non-finite values.
Results may differ from a plain program's by a relative error of at most 0.002.
Values may be sent and summed in bfloat16 or wider, within the bound.
A program may use at most 128 MiB of HBM per device.

v0:
```python
import math
import jax
import jax.numpy as jnp
from jax import lax
from jax.sharding import Mesh
from jax.sharding import PartitionSpec as P

D = 4608
FF = 36864
L = 352
DP = ("dp_0", "dp_1")


def in_blocks(array, dim, length):
    dims = array.shape
    blocks = array.reshape(*dims[:dim], length, dims[dim] // length, *dims[dim + 1 :])
    return jnp.moveaxis(blocks, dim, 0)


def sum_at_owner(array, axis, dim):
    length = lax.axis_size(axis)
    blocks = lax.all_to_all(in_blocks(array, dim, length), axis, 0, 0, tiled=True)
    return jnp.sum(blocks, axis=0)


def sent_to_all(array, axis):
    length = lax.axis_size(axis)
    return lax.all_to_all(
        jnp.broadcast_to(array[None], (length, *array.shape)), axis, 0, 0, tiled=True
    )


def over_copies(array, axis):
    everything = sent_to_all(array, axis)
    return jnp.sum(everything, axis=0)


def summed_rows(subtotal, axes):
    for axis in axes:
        subtotal = lax.psum_scatter(subtotal, axis, scatter_dimension=0, tiled=True)
    return subtotal


def on_device(hidden_act, out_grad, other_sq):
    examples_here = other_sq.shape[0]
    length = hidden_act.shape[0] // examples_here
    hidden_blocks = hidden_act.reshape(examples_here, length, hidden_act.shape[1])
    act_gram = jnp.einsum(
        "etf,esf->ets", hidden_blocks, hidden_blocks, preferred_element_type=jnp.float32
    )
    full_grad = lax.all_gather(out_grad, "tensor", axis=1, tiled=True)
    grad_blocks = full_grad.reshape(examples_here, length, full_grad.shape[1])
    act_share = sum_at_owner(act_gram, "tensor", 1)
    share_rows = act_share.shape[1]
    row_start = lax.axis_index("tensor") * share_rows
    grad_share = lax.dynamic_slice_in_dim(grad_blocks, row_start, share_rows, 1)
    grad_gram_rows = jnp.einsum(
        "etd,esd->ets", grad_share, grad_blocks, preferred_element_type=jnp.float32
    )
    layer_sq = over_copies(jnp.sum(act_share * grad_gram_rows, axis=(1, 2)), "tensor")
    clip_bound = math.sqrt(L * FF * D / 80.0)
    clip_scale = jnp.minimum(1.0, clip_bound / jnp.sqrt(other_sq + layer_sq))
    scaled_grad = (grad_blocks.astype(jnp.float32) * clip_scale[:, None, None]).astype(jnp.bfloat16)
    scaled_grad = scaled_grad.reshape(examples_here * length, full_grad.shape[1])
    contract_rows = (((0,), (0,)), ((), ()))
    return summed_rows(
        lax.dot_general(scaled_grad, hidden_act, contract_rows, preferred_element_type=jnp.float32),
        DP,
    )


def solution(mesh):
    torus = Mesh(mesh.devices.reshape(4, 2, mesh.shape["tensor"]), ("dp_0", "dp_1", "tensor"))
    in_specs = (P(DP, "tensor"), P(DP, "tensor"), P(DP))
    out_specs = P(DP, "tensor")
    return jax.shard_map(
        on_device, mesh=torus, in_specs=in_specs, out_specs=out_specs, check_vma=False
    )
```

profile of v0, /device:TPU:1, one launch (start us, length us, event | category | flops | bytes accessed | tf_op | source)
XLA Modules:
  0.0 625.2 jit_solution(8400824350638153253)
XLA Ops:
  6.5 0.0 copy-start
  6.5 0.0 all-gather.2.cloned.1.call-start
  6.5 0.7 all-gather.2.cloned.1.call-update
  7.3 1.2 copy-done
  8.5 1.8 fusion.5
  10.3 1.8 copy.13
  12.1 9.3 %all-to-all-start = ((f32[16,2,22,352]{3,1,2,0:T(2,128)}), f32[16,2,22,352]{3,1,2,0:T(2,128)}, u32[]{:S(2)}, u32[]{:S(2)}) async-start(f32[16,2,22,352]{3,1,2,0:T(2,128)} %bitcast.11), calls=%async_computation | async-start | bytes 2162688 | tf_op jit(solution)/shard_map/all_to_all | solution.py:22
  21.4 0.0 reduce-scatter.3.cloned.1.call-start
  21.4 20.4 %all-to-all-done = f32[16,2,22,352]{3,1,2,0:T(2,128)} async-done(((f32[16,2,22,352]{3,1,2,0:T(2,128)}), f32[16,2,22,352]{3,1,2,0:T(2,128)}, u32[]{:S(2)}, u32[]{:S(2)}) %all-to-all-start) | async-done | bytes 991264 | tf_op jit(solution)/shard_map/all_to_all | solution.py:22
  41.8 1.6 reduce_sum.27
  43.5 44.9 %all-gather.2.cloned.1.call-done = bf16[704,4608]{0,1:T(8,128)(2,1)} async-done(((bf16[704,288]{0,1:T(8,128)(2,1)}), bf16[704,4608]{0,1:T(8,128)(2,1)}) %all-gather.2.cloned.1.call-update) | async-done | bytes 6488080 | tf_op jit(solution)/shard_map/all_gather | solution.py:51
  88.4 9.4 %copy.14 = bf16[704,4608]{1,0:T(8,128)(2,1)} copy(bf16[704,4608]{0,1:T(8,128)(2,1)} %all-gather.2.cloned.1.call-done) | data formatting | bytes 12976128 | tf_op jit(solution)/shard_map/all_gather | solution.py:51
  97.8 4.9 fusion.2
  102.8 10.1 %all_to_all.11 = f32[16,1,2]{2,1,0:T(1,128)S(1)} all-to-all(f32[16,1,2]{2,1,0:T(1,128)S(1)} %broadcast_in_dim.2), channel_id=1, replica_groups=mesh['dp_0'=4,'dp_1'=2,'tensor'=16] {'tensor'}, dimensions={0} | all-to-all | bytes 256 | tf_op jit(solution)/shard_map/all_to_all | solution.py:28
  113.0 0.1 mul.21
  113.0 0.1 mul.22
  113.1 25.2 %fusion = f32[4608,2304]{1,0:T(8,128)} fusion(bf16[704,2304]{1,0:T(8,128)(2,1)S(1)} %copy-done, bf16[704,4608]{0,1:T(8,128)(2,1)} %all-gather.2.cloned.1.call-done, f32[704]{0:T(1024)S(1)} %mul.22), kind=kOutput, calls=%fused_computation.1 | convolution fusion | flops 14958231552 | bytes 52202240 | tf_op jit(solution)/shard_map/dot_general | solution.py:67
  138.4 0.0 reduce-scatter.3.cloned.1.call-update
  138.4 0.0 copy-start.1
  138.4 0.0 reduce-scatter.5.cloned.1.call-start
  138.4 352.2 %reduce-scatter.3.cloned.1.call-done = f32[1152,2304]{1,0:T(8,128)} async-done(((f32[4608,2304]{1,0:T(8,128)}), f32[1152,2304]{1,0:T(8,128)}) %reduce-scatter.3.cloned.1.call-update) | async-done | bytes 10616848 | tf_op jit(solution)/shard_map/reduce_scatter | solution.py:40
  490.6 0.0 reduce-scatter.5.cloned.1.call-update
  490.6 128.0 %reduce-scatter.5.cloned.1.call-done = f32[576,2304]{1,0:T(8,128)} async-done(((f32[1152,2304]{1,0:T(8,128)}), f32[576,2304]{1,0:T(8,128)}) %reduce-scatter.5.cloned.1.call-update) | async-done | bytes 5308432 | tf_op jit(solution)/shard_map/reduce_scatter | solution.py:40
  618.7 0.0 copy-done.1
  (5 shorter events, 0.1 us)
Async XLA Ops:
  6.5 1.9 copy-start
  6.5 81.9 %all-gather.2.cloned.1.call-start = ((), (), s32[]{:S(2)}) async-start(), calls=%async_computation.4 | async-start | bytes 7520256 | tf_op jit(solution)/shard_map/all_gather | solution.py:51
  12.1 29.7 %all-to-all-start = ((f32[16,2,22,352]{3,1,2,0:T(2,128)}), f32[16,2,22,352]{3,1,2,0:T(2,128)}, u32[]{:S(2)}, u32[]{:S(2)}) async-start(f32[16,2,22,352]{3,1,2,0:T(2,128)} %bitcast.11), calls=%async_computation | async-start | bytes 2162688 | tf_op jit(solution)/shard_map/all_to_all | solution.py:22
  21.4 469.2 %reduce-scatter.3.cloned.1.call-start = ((), (), s32[]{:S(2)}) async-start(), calls=%async_computation.5 | async-start | bytes 53084160 | tf_op jit(solution)/shard_map/reduce_scatter | solution.py:40
  97.8 15.1 %copy-start.2 = (f32[2]{0:T(128)S(1)}, f32[2]{0:T(128)}, u32[]{:S(2)}) copy-start(f32[2]{0:T(128)} %param.5) | copy-start | bytes 28
  138.4 480.3 %copy-start.1 = (bf16[704,2304]{1,0:T(8,128)(2,1)S(1)}, bf16[704,2304]{1,0:T(8,128)(2,1)}, u32[]{:S(2)}) copy-start(bf16[704,2304]{1,0:T(8,128)(2,1)} %param.3) | copy-start | bytes 9732100
  138.4 480.3 %reduce-scatter.5.cloned.1.call-start = ((), (), s32[]{:S(2)}) async-start(), calls=%async_computation.6 | async-start | bytes 15925248 | tf_op jit(solution)/shard_map/reduce_scatter | solution.py:40
Sparse Core Ops, SparseCore 0:
  9.7 78.6 all-gather.1
  138.5 352.0 reduce-scatter.2
  493.0 125.5 reduce-scatter.4
where the time goes:
time: 626 us; the launch traced here: 625 us
  waiting for transfers between devices  546 us (87%)
  matrix products  32 us (5%)
  between operations  13.1 us (2%)
  local copies, waits for them, and re-layouts  12.6 us (2%)
  blocking collectives  10.1 us (2%)
  starting transfers between devices  9.37 us (1%)
    reduce_scatter x2, waiting for transfers between devices, summed_rows(): subtotal = lax.psum_scatter(subtotal, axis, scatter_dimension=0, tiled=True)  480 us
    all_gather x1, waiting for transfers between devices, on_device(): full_grad = lax.all_gather(out_grad, 'tensor', axis=1, tiled=True)  44.9 us
    dot_general x1, matrix products, on_device(): lax.dot_general(scaled_grad, hidden_act, contract_rows, preferred_element...  25.2 us
    all_to_all x1, waiting for transfers between devices, sum_at_owner(): lax.all_to_all(in_blocks(array, dim, length), axis, 0, 0, tiled=True)  20.4 us
  transfers between devices with their start and end apart: 4, of which 4 were waited for; matrix products, arithmetic and copies ran while one was open for 1% of the time, Pallas kernels for 0%

commit v1 on v0

--- a/solution.py
+++ b/solution.py
@@ -48,7 +48,9 @@
     act_gram = jnp.einsum(
         "etf,esf->ets", hidden_blocks, hidden_blocks, preferred_element_type=jnp.float32
     )
-    full_grad = lax.all_gather(out_grad, "tensor", axis=1, tiled=True)
+    full_grad = jnp.concatenate(
+        lax.all_to_all(jnp.stack([out_grad] * lax.axis_size("tensor")), "tensor", 0, 0), axis=1
+    )
     grad_blocks = full_grad.reshape(examples_here, length, full_grad.shape[1])
     act_share = sum_at_owner(act_gram, "tensor", 1)
     share_rows = act_share.shape[1]

time: 626 us -> 724 us (1.16)
  waiting for transfers between devices: 546 us -> 585 us
  blocking collectives: 10.1 us -> 45.6 us
  local copies, waits for them, and re-layouts: 12.6 us -> 40.9 us
    all_to_all x1, waiting for transfers between devices: 20.4 us -> 105 us  [on_device(): lax.all_to_all(jnp.stack([out_grad] * lax.axis_size('tensor')), 'tensor',...]
    all_gather x1 -> x0, waiting for transfers between devices: 44.9 us -> none  [on_device(): full_grad = lax.all_gather(out_grad, 'tensor', axis=1, tiled=True)]
    another operation x0 -> x3, local copies, waits for them, and re-layouts: none -> 37.9 us  [the longest x2 34.3 us: on_device(): grad_blocks = full_grad.reshape(examples_here, length, full_grad.shape[1])]
    all_to_all x0 -> x1, blocking collectives: none -> 27.3 us  [sum_at_owner(): lax.all_to_all(in_blocks(array, dim, length), axis, 0, 0, tiled=True)]
    all_gather x1 -> x0, local copies, waits for them, and re-layouts: 9.44 us -> none  [on_device(): full_grad = lax.all_gather(out_grad, 'tensor', axis=1, tiled=True)]
    all_to_all x1, blocking collectives: 10.1 us -> 18.3 us  [sent_to_all(): lax.all_to_all(jnp.broadcast_to(array[None], (length, *array.shape)), axi...]
  transfers between devices with their start and end apart: 4 -> 3, of which waited for: 4 -> 3; matrix products, arithmetic and copies ran while one was open for 1% -> 0% of each run, Pallas kernels for 0% -> 0%
where the time goes in v1:
time: 724 us; the launch traced here: 723 us
  waiting for transfers between devices  585 us (81%)
  blocking collectives  45.6 us (6%)
  local copies, waits for them, and re-layouts  40.9 us (6%)
  matrix products  32 us (4%)
  between operations  13.5 us (2%)
    reduce_scatter x2, waiting for transfers between devices, summed_rows(): subtotal = lax.psum_scatter(subtotal, axis, scatter_dimension=0, tiled=True)  480 us
    all_to_all x1, waiting for transfers between devices, on_device(): lax.all_to_all(jnp.stack([out_grad] * lax.axis_size('tensor')), 'tensor',...  105 us
    another operation x2, local copies, waits for them, and re-layouts, on_device(): grad_blocks = full_grad.reshape(examples_here, length, full_grad.shape[1])  34.3 us
    all_to_all x1, blocking collectives, sum_at_owner(): lax.all_to_all(in_blocks(array, dim, length), axis, 0, 0, tiled=True)  27.3 us
    dot_general x1, matrix products, on_device(): lax.dot_general(scaled_grad, hidden_act, contract_rows, preferred_element...  25.2 us
    all_to_all x1, blocking collectives, sent_to_all(): lax.all_to_all(jnp.broadcast_to(array[None], (length, *array.shape)), axi...  18.3 us
  transfers between devices with their start and end apart: 3, of which 3 were waited for; matrix products, arithmetic and copies ran while one was open for 0% of the time, Pallas kernels for 0%

profile of v1, /device:TPU:1, one launch (start us, length us, event | category | flops | bytes accessed | tf_op | source)
XLA Modules:
  0.0 723.2 jit_solution(10454587081359199828)
XLA Ops:
  6.5 0.0 copy-start
  6.5 1.9 copy-done
  8.5 1.8 fusion.7
  10.3 0.8 copy.16
  11.1 27.3 %all_to_all.16 = f32[16,2,22,352]{3,1,2,0:T(2,128)} all-to-all(f32[16,2,22,352]{3,1,2,0:T(2,128)S(1)} %bitcast.15), channel_id=1, replica_groups=mesh['dp_0'=4,'dp_1'=2,'tensor'=16] {'tensor'}, dimensions={0} | all-to-all | bytes 1982464 | tf_op jit(solution)/shard_map/all_to_all | solution.py:22
  38.5 0.0 copy-done.2
  38.5 3.6 stack.2
  42.1 4.8 all-to-all-start
  46.9 0.0 reduce-scatter.3.cloned.1.call-start
  46.9 1.6 reduce_sum.27
  48.6 104.7 %all-to-all-done = bf16[16,704,288]{1,2,0:T(8,128)(2,1)} async-done(((bf16[16,704,288]{1,2,0:T(8,128)(2,1)}), bf16[16,704,288]{1,2,0:T(8,128)(2,1)}, u32[]{:S(2)}, u32[]{:S(2)}) %all-to-all-start) | async-done | bytes 6488096 | tf_op jit(solution)/shard_map/all_to_all | solution.py:52
  153.3 16.3 %reshape_reshape.3 = bf16[2,352,4608]{1,0,2:T(2,128)(2,1)} reshape(bf16[704,16,288]{0,2,1:T(8,128)(2,1)} %bitcast) | data formatting | bytes 12976128 | tf_op jit(solution)/shard_map/reshape;reshape | solution.py:54
  169.6 18.0 %copy.17 = bf16[2,352,4608]{2,1,0:T(8,128)(2,1)} copy(bf16[2,352,4608]{1,0,2:T(2,128)(2,1)} %reshape_reshape.3) | data formatting | bytes 12976128 | tf_op jit(solution)/shard_map/reshape;reshape | solution.py:54
  187.6 4.9 fusion.4
  192.6 18.3 %all_to_all.17 = f32[16,1,2]{2,1,0:T(1,128)S(1)} all-to-all(f32[16,1,2]{2,1,0:T(1,128)S(1)} %broadcast_in_dim.2), channel_id=1, replica_groups=mesh['dp_0'=4,'dp_1'=2,'tensor'=16] {'tensor'}, dimensions={0} | all-to-all | bytes 256 | tf_op jit(solution)/shard_map/all_to_all | solution.py:28
  210.9 0.1 mul.21
  211.0 0.1 mul.22
  211.1 25.2 %fusion.1 = f32[4608,2304]{1,0:T(8,128)} fusion(bf16[704,2304]{1,0:T(8,128)(2,1)S(1)} %copy-done, bf16[704,4608]{0,1:T(8,128)(2,1)} %bitcast.5, f32[704]{0:T(1024)S(1)} %mul.22), kind=kOutput, calls=%fused_computation.2 | convolution fusion | flops 14958231552 | bytes 52202240 | tf_op jit(solution)/shard_map/dot_general | solution.py:69
  236.3 0.0 reduce-scatter.3.cloned.1.call-update
  236.3 0.0 copy-start.1
  236.3 0.0 reduce-scatter.5.cloned.1.call-start
  236.4 351.9 %reduce-scatter.3.cloned.1.call-done = f32[1152,2304]{1,0:T(8,128)} async-done(((f32[4608,2304]{1,0:T(8,128)}), f32[1152,2304]{1,0:T(8,128)}) %reduce-scatter.3.cloned.1.call-update) | async-done | bytes 10616848 | tf_op jit(solution)/shard_map/reduce_scatter | solution.py:40
  588.3 0.0 reduce-scatter.5.cloned.1.call-update
  588.3 128.0 %reduce-scatter.5.cloned.1.call-done = f32[576,2304]{1,0:T(8,128)} async-done(((f32[1152,2304]{1,0:T(8,128)}), f32[576,2304]{1,0:T(8,128)}) %reduce-scatter.5.cloned.1.call-update) | async-done | bytes 5308432 | tf_op jit(solution)/shard_map/reduce_scatter | solution.py:40
  (7 shorter events, 0.1 us)
Async XLA Ops:
  6.5 1.9 copy-start
  8.5 30.0 %copy-start.2 = (bf16[704,288]{0,1:T(8,128)(2,1)S(1)}, bf16[704,288]{0,1:T(8,128)(2,1)}, u32[]{:S(2)}) copy-start(bf16[704,288]{0,1:T(8,128)(2,1)} %param.4) | copy-start | bytes 1216516
  42.1 111.2 %all-to-all-start = ((bf16[16,704,288]{1,2,0:T(8,128)(2,1)}), bf16[16,704,288]{1,2,0:T(8,128)(2,1)}, u32[]{:S(2)}, u32[]{:S(2)}) async-start(bf16[16,704,288]{1,2,0:T(8,128)(2,1)} %stack.2), calls=%async_computation | async-start | bytes 14155776 | tf_op jit(solution)/shard_map/all_to_all | solution.py:52
  46.9 541.4 %reduce-scatter.3.cloned.1.call-start = ((), (), s32[]{:S(2)}) async-start(), calls=%async_computation.5 | async-start | bytes 53084160 | tf_op jit(solution)/shard_map/reduce_scatter | solution.py:40
  187.6 23.3 %copy-start.3 = (f32[2]{0:T(128)S(1)}, f32[2]{0:T(128)}, u32[]{:S(2)}) copy-start(f32[2]{0:T(128)} %param.5) | copy-start | bytes 28
  236.3 480.0 %copy-start.1 = (bf16[704,2304]{1,0:T(8,128)(2,1)S(1)}, bf16[704,2304]{1,0:T(8,128)(2,1)}, u32[]{:S(2)}) copy-start(bf16[704,2304]{1,0:T(8,128)(2,1)} %param.3) | copy-start | bytes 9732100
  236.3 480.0 %reduce-scatter.5.cloned.1.call-start = ((), (), s32[]{:S(2)}) async-start(), calls=%async_computation.6 | async-start | bytes 15925248 | tf_op jit(solution)/shard_map/reduce_scatter | solution.py:40
Sparse Core Ops, SparseCore 0:
  236.4 351.7 reduce-scatter.2
  590.7 125.6 reduce-scatter.4
